TPU v7x, 32 devices: a whole 2x2x4 slice. The times are simulated.
32 devices in a mesh: job: 2 (over y), ta: 4 (over z), xyz: 2 (over x), src: 2 (over core).
Axes of the slice: x: 2, y: 2, z: 4, core: 2. Of those that a mesh axis runs over, the one named last changes fastest.
Arguments:
- spinors: float32 [64, 8, 2, 8, 3, 512], P('src', 'ta', None, 'job', None, 'xyz'), parts along dimension 3, may hold values from -6 to 6
- eigvecs: float32 [8, 256, 2, 3, 512], P('ta', 'job', None, None, 'xyz'), parts along dimension 1, may hold values from -0.109375 to 0.109375
- group_of: int32 [8], replicated, may hold values from 0 to 3, as said below
- source_ids: int32 [64], P('src'), may hold values from 0 to 63, as said below
Outputs:
- perambulator: float32 [8, 2, 8, 64, 128], P('ta', None, 'job', 'src', 'xyz'), parts along dimension 2
There are 2 independent parts, one for each index of `job`. A program takes and returns all parts, laid end to end along the dimension named above; an argument that names none is the same for every part. Nothing has to cross between parts.
Inputs may be any that keep to these rules, and one draw needn't show every extreme that they name: `group_of`: every group number appears exactly 2 times. `source_ids`: the 32 entries held by index i of src are a permutation of i * 32 to (i + 1) * 32 - 1.
All inputs are finite; a program needn't handle non-finite values.
Results may differ from a plain program's by a relative error of at most 0.00007.
Values sent between devices are 32-bit elements; how exact they have to be, the bound alone decides.
A program may use at most 64 MiB of HBM per device.

v0:
```python
import jax
import jax.numpy as jnp
from jax import lax
from jax.sharding import PartitionSpec as P


def contract_pair(vectors, spinor):
    vector_real = vectors[:, :, 0]
    vector_imag = vectors[:, :, 1]
    spinor_real = spinor[:, :, 0]
    spinor_imag = spinor[:, :, 1]

    def contract(left_side, right_side):
        return jnp.einsum(
            "tkcx,ntscx->tsnk", left_side, right_side, precision=lax.Precision.HIGHEST
        )

    real_part = contract(vector_real, spinor_real) + contract(vector_imag, spinor_imag)
    imag_part = contract(vector_real, spinor_imag) - contract(vector_imag, spinor_real)
    return jnp.stack([real_part, imag_part], axis=1)


def local(spinors, eigvecs, group_of, source_ids):
    extent = group_of.shape[0]
    sort_keys = group_of * extent + jnp.arange(extent, dtype=jnp.int32)
    ordering = jnp.argsort(sort_keys)
    spread = lax.all_to_all(spinors, "ta", split_axis=0, concat_axis=1, tiled=True)
    grouped = jnp.take(spread, ordering, axis=1)
    regrouped = lax.all_to_all(grouped, "ta", split_axis=1, concat_axis=0, tiled=True)
    partial_sums = contract_pair(eigvecs, regrouped)
    summed = lax.psum_scatter(partial_sums, "xyz", scatter_dimension=4, tiled=True)
    inverse = jnp.argsort(source_ids)
    return jnp.take(summed, inverse, axis=3)


def solution(mesh):
    in_specs = (
        P("src", "ta", None, "job", None, "xyz"),
        P("ta", "job", None, None, "xyz"),
        P(),
        P("src"),
    )
    out_specs = P("ta", None, "job", "src", "xyz")
    return jax.shard_map(local, mesh=mesh, in_specs=in_specs, out_specs=out_specs, check_vma=False)
```

profile of v0, /device:TPU:0, one launch (start us, length us, event | category | flops | bytes accessed | tf_op | source)
XLA Modules:
  0.0 120.4 jit_solution(10331369571114613765)
XLA Ops:
  6.5 0.0 copy-start
  6.5 6.5 %all-to-all-start = ((f32[32,2,2,4,3,256]{5,3,4,2,1,0:T(4,128)}), f32[32,2,2,4,3,256]{5,3,4,2,1,0:T(4,128)S(1)}, u32[]{:S(2)}, u32[]{:S(2)}) async-start(f32[32,2,2,4,3,256]{5,3,4,2,1,0:T(4,128)} %param.4), calls=%async_computation | async-start | bytes 3145728 | tf_op jit(solution)/shard_map/all_to_all | solution.py:27
  13.0 0.0 copy-done
  13.0 1.0 sort.35
  14.0 36.0 %all-to-all-done = f32[32,2,2,4,3,256]{5,3,4,2,1,0:T(4,128)S(1)} async-done(((f32[32,2,2,4,3,256]{5,3,4,2,1,0:T(4,128)}), f32[32,2,2,4,3,256]{5,3,4,2,1,0:T(4,128)S(1)}, u32[]{:S(2)}, u32[]{:S(2)}) %all-to-all-start) | async-done | bytes 1572896 | tf_op jit(solution)/shard_map/all_to_all | solution.py:27
  50.0 0.9 copy.55
  50.9 0.2 copy.29
  51.1 0.7 gather_fusion
  51.7 1.4 %select_bitcast_fusion = f32[8,8,2,4,3,256]{5,0,4,3,2,1:T(8,128)} fusion(f32[8,8,2,4,3,256]{5,1,4,3,2,0:T(8,128)S(1)} %gather_fusion, pred[8]{0:T(512)(128)(4,1)S(1)} %compare_and_fusion), kind=kLoop, calls=%fused_computation.4 | loop fusion | flops 393216 | bytes 3145736 | tf_op jit(solution)/shard_map/jit(_take)/select_n | solution.py:28
  53.1 0.0 copy-start.1
  53.2 3.7 %all-to-all-start.1 = ((f32[8,8,2,4,3,256]{5,0,4,3,2,1:T(8,128)}), f32[8,8,2,4,3,256]{5,0,4,3,2,1:T(8,128)S(1)}, u32[]{:S(2)}, u32[]{:S(2)}) async-start(f32[8,8,2,4,3,256]{5,0,4,3,2,1:T(8,128)} %select_bitcast_fusion), calls=%async_computation.1 | async-start | bytes 3145728 | tf_op jit(solution)/shard_map/all_to_all | solution.py:29
  56.9 0.0 reduce-scatter.4.cloned.1.call-start
  56.9 0.0 copy-done.1
  56.9 1.6 %sort.34 = (s32[32]{0:T(128)}, s32[32]{0:T(128)S(1)}) sort(s32[32]{0:T(128)S(1)} %copy-done.1, s32[32]{0:T(128)S(1)} %iota.11), dimensions={0}, to_apply=%region_0.0 | sort | flops 160 | bytes 512 | tf_op jit(solution)/shard_map/jit(argsort)/sort | solution.py:32
  58.5 3.4 %fusion.4 = (f32[2,128,1,3,256]{4,2,3,1,0:T(1,128)S(1)}, f32[2,128,1,3,256]{4,2,3,1,0:T(1,128)S(1)}) fusion(f32[2,128,2,3,256]{4,2,3,1,0:T(2,128)} %param.5), kind=kLoop, calls=%fused_computation.26 | loop fusion | bytes 3145728 | tf_op jit(solution)/shard_map/slice | solution.py:8
  61.9 31.4 %all-to-all-done.1 = f32[8,8,2,4,3,256]{5,0,4,3,2,1:T(8,128)S(1)} async-done(((f32[8,8,2,4,3,256]{5,0,4,3,2,1:T(8,128)}), f32[8,8,2,4,3,256]{5,0,4,3,2,1:T(8,128)S(1)}, u32[]{:S(2)}, u32[]{:S(2)}) %all-to-all-start.1) | async-done | bytes 1572896 | tf_op jit(solution)/shard_map/all_to_all | solution.py:29
  93.3 0.2 copy.54
  93.6 0.9 convolution_bitcast_fusion.2
  94.5 0.9 convolution_bitcast_fusion
  95.3 0.9 fusion.1
  96.2 0.9 fusion.3
  97.1 0.6 copy.41
  97.7 1.7 %reshape.34 = f32[128,512]{1,0:T(8,128)} reshape(f32[128,2,2,4,32]{4,3,2,1,0:T(4,128)S(1)} %bitcast.76) | data formatting | bytes 524288
  99.4 0.0 reduce-scatter.4.cloned.1.call-update
  99.5 11.0 %reduce-scatter.4.cloned.1.call-done = f32[64,512]{1,0:T(8,128)} async-done(((f32[128,512]{1,0:T(8,128)}), f32[64,512]{1,0:T(8,128)}) %reduce-scatter.4.cloned.1.call-update) | async-done | bytes 131088
  110.4 1.2 reshape.35
  111.6 0.3 copy.33
  111.9 0.7 gather_fusion.1
  112.7 0.1 select_bitcast_fusion.1
  112.8 0.8 copy.34
  (10 shorter events, 0.1 us)
Async XLA Ops:
  6.5 6.5 %copy-start = (s32[8]{0:T(128)S(1)}, s32[8]{0:T(128)}, u32[]{:S(2)}) copy-start(s32[8]{0:T(128)} %param.6) | copy-start | bytes 100
  6.5 43.4 %all-to-all-start = ((f32[32,2,2,4,3,256]{5,3,4,2,1,0:T(4,128)}), f32[32,2,2,4,3,256]{5,3,4,2,1,0:T(4,128)S(1)}, u32[]{:S(2)}, u32[]{:S(2)}) async-start(f32[32,2,2,4,3,256]{5,3,4,2,1,0:T(4,128)} %param.4), calls=%async_computation | async-start | bytes 3145728 | tf_op jit(solution)/shard_map/all_to_all | solution.py:27
  53.1 3.8 %copy-start.1 = (s32[32]{0:T(128)S(1)}, s32[32]{0:T(128)}, u32[]{:S(2)}) copy-start(s32[32]{0:T(128)} %param.7) | copy-start | bytes 388
  53.2 40.2 %all-to-all-start.1 = ((f32[8,8,2,4,3,256]{5,0,4,3,2,1:T(8,128)}), f32[8,8,2,4,3,256]{5,0,4,3,2,1:T(8,128)S(1)}, u32[]{:S(2)}, u32[]{:S(2)}) async-start(f32[8,8,2,4,3,256]{5,0,4,3,2,1:T(8,128)} %select_bitcast_fusion), calls=%async_computation.1 | async-start | bytes 3145728 | tf_op jit(solution)/shard_map/all_to_all | solution.py:29
  56.9 53.6 %reduce-scatter.4.cloned.1.call-start = ((), (), s32[]{:S(2)}) async-start(), calls=%async_computation.3 | async-start | bytes 393216
Sparse Core Ops, SparseCore 0:
  99.5 10.8 reduce-scatter.3
where the time goes:
time: 121 us; the launch traced here: 120 us
  waiting for transfers between devices  78.4 us (65%)
  between operations  13.6 us (11%)
  local copies, waits for them, and re-layouts  10.6 us (9%)
  starting transfers between devices  10.2 us (8%)
  other arithmetic  4.16 us (3%)
  matrix products  3.51 us (3%)
    all_to_all x1, waiting for transfers between devices, local(): lax.all_to_all(spinors, 'ta', split_axis=0, concat_axis=1, tiled=True)  36 us
    all_to_all x1, waiting for transfers between devices, local(): lax.all_to_all(grouped, 'ta', split_axis=1, concat_axis=0, tiled=True)  31.4 us
    unnamed x2, waiting for transfers between devices  11 us
    all_to_all x1, starting transfers between devices, local(): lax.all_to_all(spinors, 'ta', split_axis=0, concat_axis=1, tiled=True)  6.48 us
    all_to_all x1, starting transfers between devices, local(): lax.all_to_all(grouped, 'ta', split_axis=1, concat_axis=0, tiled=True)  3.69 us
    dot_general x4, matrix products, contract(): jnp.einsum('tkcx,ntscx->tsnk', left_side, right_side, precision=lax.Preci...  3.51 us
    unnamed x7, local copies, waits for them, and re-layouts  3.43 us
    slice x1, local copies, waits for them, and re-layouts, contract_pair(): vector_real = vectors[:, :, 0]  3.37 us
  transfers between devices with their start and end apart: 3, of which 3 were waited for; matrix products, arithmetic and copies ran while one was open for 5% of the time, Pallas kernels for 0%

commit v1 on v0

--- a/solution.py
+++ b/solution.py
@@ -26,7 +26,25 @@
     ordering = jnp.argsort(sort_keys)
     spread = lax.all_to_all(spinors, "ta", split_axis=0, concat_axis=1, tiled=True)
     grouped = jnp.take(spread, ordering, axis=1)
-    regrouped = lax.all_to_all(grouped, "ta", split_axis=1, concat_axis=0, tiled=True)
+
+    def perform_modes(field):
+        f_now, far_arr = (lax.psum(1, "ta"), lax.axis_index("ta"))
+        now = field.shape[1] // f_now
+        f_next = list(field.shape)
+        f_next[1] = now
+        response = f_next[0]
+        f_next[0] = response * f_now
+        k_now = jnp.zeros(f_next, field.dtype)
+        for s in range(f_now):
+            current_arr = lax.dynamic_slice_in_dim(field, (far_arr ^ s) * now, now, axis=1)
+            if s:
+                current_arr = lax.ppermute(current_arr, "ta", [(pp, pp ^ s) for pp in range(f_now)])
+            k_now = lax.dynamic_update_slice_in_dim(
+                k_now, current_arr, (far_arr ^ s) * response, axis=0
+            )
+        return k_now
+
+    regrouped = perform_modes(grouped)
     partial_sums = contract_pair(eigvecs, regrouped)
     summed = lax.psum_scatter(partial_sums, "xyz", scatter_dimension=4, tiled=True)
     inverse = jnp.argsort(source_ids)

time: 121 us -> 115 us (0.950)
  waiting for transfers between devices: 78.4 us -> 72.9 us
    all_to_all x1 -> x0, waiting for transfers between devices: 31.4 us -> none  [local(): lax.all_to_all(grouped, 'ta', split_axis=1, concat_axis=0, tiled=True)]
    ppermute x0 -> x3, waiting for transfers between devices: none -> 20.3 us  [perform_modes(): lax.ppermute(current_arr, 'ta', [(pp, pp ^ s) for pp in range(f_now)])]
    unnamed x2, waiting for transfers between devices: 11 us -> 16.7 us
    ppermute x0 -> x3, starting transfers between devices: none -> 4.44 us  [perform_modes(): lax.ppermute(current_arr, 'ta', [(pp, pp ^ s) for pp in range(f_now)])]
    all_to_all x1 -> x0, starting transfers between devices: 3.69 us -> none  [local(): lax.all_to_all(grouped, 'ta', split_axis=1, concat_axis=0, tiled=True)]
    dynamic_update_slice x0 -> x4, local copies, waits for them, and re-layouts: none -> 2.17 us  [perform_modes(): lax.dynamic_update_slice_in_dim(k_now, current_arr, (far_arr ^ s) * respo...]
    slice x1, local copies, waits for them, and re-layouts: 3.37 us -> 1.21 us  [contract_pair(): vector_real = vectors[:, :, 0]]
    unnamed x7 -> x11, local copies, waits for them, and re-layouts: 3.43 us -> 3.44 us
  transfers between devices with their start and end apart: 3 -> 5, of which waited for: 3 -> 4; matrix products, arithmetic and copies ran while one was open for 5% -> 5% of each run, Pallas kernels for 0% -> 0%
where the time goes in v1:
time: 115 us
  waiting for transfers between devices  72.9 us (63%)
  between operations  13.6 us (12%)
  starting transfers between devices  10.9 us (9%)
  local copies, waits for them, and re-layouts  10.7 us (9%)
  matrix products  3.51 us (3%)
  other arithmetic  2.99 us (3%)
    all_to_all x1, waiting for transfers between devices, local(): lax.all_to_all(spinors, 'ta', split_axis=0, concat_axis=1, tiled=True)  36 us
    ppermute x3, waiting for transfers between devices, perform_modes(): lax.ppermute(current_arr, 'ta', [(pp, pp ^ s) for pp in range(f_now)])  20.3 us
    unnamed x2, waiting for transfers between devices  16.7 us
    all_to_all x1, starting transfers between devices, local(): lax.all_to_all(spinors, 'ta', split_axis=0, concat_axis=1, tiled=True)  6.48 us
    ppermute x3, starting transfers between devices, perform_modes(): lax.ppermute(current_arr, 'ta', [(pp, pp ^ s) for pp in range(f_now)])  4.44 us
    dot_general x4, matrix products, contract(): jnp.einsum('tkcx,ntscx->tsnk', left_side, right_side, precision=lax.Preci...  3.51 us
    unnamed x11, local copies, waits for them, and re-layouts  3.44 us
  transfers between devices with their start and end apart: 5, of which 4 were waited for; matrix products, arithmetic and copies ran while one was open for 5% of the time, Pallas kernels for 0%

profile of v1, /device:TPU:0, one launch (start us, length us, event | category | flops | bytes accessed | tf_op | source)
XLA Modules:
  0.0 114.7 jit_solution(5272722936706682597)
XLA Ops:
  6.5 0.0 copy-start.2
  6.5 6.5 %all-to-all-start = ((f32[32,2,2,4,3,256]{5,3,4,2,1,0:T(4,128)}), f32[32,2,2,4,3,256]{5,3,4,2,1,0:T(4,128)S(1)}, u32[]{:S(2)}, u32[]{:S(2)}) async-start(f32[32,2,2,4,3,256]{5,3,4,2,1,0:T(4,128)} %param.4), calls=%async_computation | async-start | bytes 3145728 | tf_op jit(solution)/shard_map/all_to_all | solution.py:27
  13.0 0.0 reduce-scatter.4.cloned.1.call-start
  13.0 0.0 copy-done.2
  13.0 1.0 sort.35
  14.0 36.0 %all-to-all-done = f32[32,2,2,4,3,256]{5,3,4,2,1,0:T(4,128)S(1)} async-done(((f32[32,2,2,4,3,256]{5,3,4,2,1,0:T(4,128)}), f32[32,2,2,4,3,256]{5,3,4,2,1,0:T(4,128)S(1)}, u32[]{:S(2)}, u32[]{:S(2)}) %all-to-all-start) | async-done | bytes 1572896 | tf_op jit(solution)/shard_map/all_to_all | solution.py:27
  50.0 0.9 copy.54
  50.9 0.2 copy.29
  51.1 0.7 gather_fusion
  51.7 0.2 copy_select_fusion
  52.0 0.0 copy-start
  52.0 0.0 copy-start.1
  52.0 0.1 dynamic-slice_bitcast_fusion
  52.1 0.1 collective-permute-start
  52.2 2.0 %collective-permute-start.1 = (f32[8,2,2,4,3,256]{5,0,4,3,1,2:T(8,128)S(1)}, f32[8,2,2,4,3,256]{5,0,4,3,1,2:T(8,128)S(1)}, u32[]{:S(2)}, u32[]{:S(2)}) collective-permute-start(f32[8,2,2,4,3,256]{5,0,4,3,1,2:T(8,128)S(1)} %get-tuple-element.12), channel_id=1, source_target_pairs={{0,8},{4,12},{8,0},{12,4},{1,9},{5,13},{9,1},{13,5},{2,10},{6,14},... | collective-permute-start | bytes 1179656 | tf_op jit(solution)/shard_map/ppermute | solution.py:41
  54.2 0.0 copy-done
  54.2 0.0 copy-start.3
  54.2 2.4 %collective-permute-start.2 = (f32[8,2,2,4,3,256]{5,0,4,3,1,2:T(8,128)S(1)}, f32[8,2,2,4,3,256]{5,0,4,3,1,2:T(8,128)S(1)}, u32[]{:S(2)}, u32[]{:S(2)}) collective-permute-start(f32[8,2,2,4,3,256]{5,0,4,3,1,2:T(8,128)S(1)} %get-tuple-element.11), channel_id=1, source_target_pairs={{0,12},{4,8},{8,4},{12,0},{1,13},{5,9},{9,5},{13,1},{2,14},{6,10},... | collective-permute-start | bytes 1179656 | tf_op jit(solution)/shard_map/ppermute | solution.py:41
  56.6 0.0 copy-done.1
  56.6 1.2 %fusion.4 = (f32[2,128,1,3,256]{4,2,3,1,0:T(1,128)S(1)}, f32[2,128,1,3,256]{4,2,3,1,0:T(1,128)S(1)}) fusion(f32[2,128,2,3,256]{4,2,3,1,0:T(2,128)S(1)} %copy-done.1), kind=kLoop, calls=%fused_computation.32 | loop fusion | bytes 3145728 | tf_op jit(solution)/shard_map/slice | solution.py:8
  57.8 0.0 copy-done.3
  57.8 1.6 %sort.34 = (s32[32]{0:T(128)}, s32[32]{0:T(128)S(1)}) sort(s32[32]{0:T(128)S(1)} %copy-done.3, s32[32]{0:T(128)S(1)} %iota.11), dimensions={0}, to_apply=%region_0.0 | sort | flops 160 | bytes 512 | tf_op jit(solution)/shard_map/jit(argsort)/sort | solution.py:50
  59.5 0.2 broadcast_in_dim.28
  59.6 1.0 bitcast_dynamic-update-slice_fusion
  60.7 9.3 %collective-permute-done = f32[8,2,2,4,3,256]{5,0,4,3,1,2:T(8,128)} collective-permute-done((f32[8,2,2,4,3,256]{5,0,4,3,1,2:T(8,128)S(1)}, f32[8,2,2,4,3,256]{5,0,4,3,1,2:T(8,128)}, u32[]{:S(2)}, u32[]{:S(2)}) %collective-permute-start) | collective-permute-done | bytes 393248 | tf_op jit(solution)/shard_map/ppermute | solution.py:41
  70.0 1.0 constant_dynamic-update-slice_fusion.1
  71.1 11.0 %collective-permute-done.1 = f32[8,2,2,4,3,256]{5,0,4,3,1,2:T(8,128)S(1)} collective-permute-done((f32[8,2,2,4,3,256]{5,0,4,3,1,2:T(8,128)S(1)}, f32[8,2,2,4,3,256]{5,0,4,3,1,2:T(8,128)S(1)}, u32[]{:S(2)}, u32[]{:S(2)}) %collective-permute-start.1) | collective-permute-done | bytes 393248 | tf_op jit(solution)/shard_map/ppermute | solution.py:41
  82.1 0.0 collective-permute-done.2
  82.1 0.9 convolution_bitcast_fusion.2
  83.0 0.9 convolution_bitcast_fusion
  83.9 0.9 fusion.1
  84.8 0.9 fusion.3
  85.7 0.6 copy.41
  86.3 1.7 %reshape.34 = f32[128,512]{1,0:T(8,128)} reshape(f32[128,2,2,4,32]{4,3,2,1,0:T(4,128)S(1)} %bitcast.71) | data formatting | bytes 524288
  88.0 0.0 reduce-scatter.4.cloned.1.call-update
  88.0 16.6 %reduce-scatter.4.cloned.1.call-done = f32[64,512]{1,0:T(8,128)} async-done(((f32[128,512]{1,0:T(8,128)}), f32[64,512]{1,0:T(8,128)}) %reduce-scatter.4.cloned.1.call-update) | async-done | bytes 131088
  104.7 1.2 %reshape.35 = f32[64,2,2,4,32]{4,3,2,1,0:T(4,128)S(1)} reshape(f32[64,512]{1,0:T(8,128)} %reduce-scatter.4.cloned.1.call-done) | data formatting | bytes 262144
  105.8 0.3 copy.33
  106.2 0.7 gather_fusion.1
  106.9 0.1 select_bitcast_fusion
  107.0 0.8 copy.34
  (12 shorter events, 0.1 us)
Async XLA Ops:
  6.5 6.5 %copy-start.2 = (s32[8]{0:T(128)S(1)}, s32[8]{0:T(128)}, u32[]{:S(2)}) copy-start(s32[8]{0:T(128)} %param.6) | copy-start | bytes 100
  6.5 43.4 %all-to-all-start = ((f32[32,2,2,4,3,256]{5,3,4,2,1,0:T(4,128)}), f32[32,2,2,4,3,256]{5,3,4,2,1,0:T(4,128)S(1)}, u32[]{:S(2)}, u32[]{:S(2)}) async-start(f32[32,2,2,4,3,256]{5,3,4,2,1,0:T(4,128)} %param.4), calls=%async_computation | async-start | bytes 3145728 | tf_op jit(solution)/shard_map/all_to_all | solution.py:27
  13.0 91.7 %reduce-scatter.4.cloned.1.call-start = ((), (), s32[]{:S(2)}) async-start(), calls=%async_computation.2 | async-start | bytes 393216
  52.0 2.2 %copy-start = (f32[8,8,2,4,3,256]{5,1,4,3,0,2:T(8,128)}, f32[8,8,2,4,3,256]{5,1,4,3,0,2:T(8,128)S(1)}, u32[]{:S(2)}) copy-start(f32[8,8,2,4,3,256]{5,1,4,3,0,2:T(8,128)S(1)} %copy_select_fusion) | copy-start | bytes 4718596
  52.0 4.6 %copy-start.1 = (f32[2,128,2,3,256]{4,2,3,1,0:T(2,128)S(1)}, f32[2,128,2,3,256]{4,2,3,1,0:T(2,128)}, u32[]{:S(2)}) copy-start(f32[2,128,2,3,256]{4,2,3,1,0:T(2,128)} %param.5) | copy-start | bytes 4718596
  52.1 17.9 %collective-permute-start = (f32[8,2,2,4,3,256]{5,0,4,3,1,2:T(8,128)S(1)}, f32[8,2,2,4,3,256]{5,0,4,3,1,2:T(8,128)}, u32[]{:S(2)}, u32[]{:S(2)}) collective-permute-start(f32[8,2,2,4,3,256]{5,0,4,3,1,2:T(8,128)S(1)} %get-tuple-element.13), channel_id=1, source_target_pairs={{0,4},{4,0},{8,12},{12,8},{1,5},{5,1},{9,13},{13,9},{2,6},{6,2},{1... | collective-permute-start | bytes 1179656 | tf_op jit(solution)/shard_map/ppermute | solution.py:41
  52.2 29.8 %collective-permute-start.1 = (f32[8,2,2,4,3,256]{5,0,4,3,1,2:T(8,128)S(1)}, f32[8,2,2,4,3,256]{5,0,4,3,1,2:T(8,128)S(1)}, u32[]{:S(2)}, u32[]{:S(2)}) collective-permute-start(f32[8,2,2,4,3,256]{5,0,4,3,1,2:T(8,128)S(1)} %get-tuple-element.12), channel_id=1, source_target_pairs={{0,8},{4,12},{8,0},{12,4},{1,9},{5,13},{9,1},{13,5},{2,10},{6,14},... | collective-permute-start | bytes 1179656 | tf_op jit(solution)/shard_map/ppermute | solution.py:41
  54.2 3.6 %copy-start.3 = (s32[32]{0:T(128)S(1)}, s32[32]{0:T(128)}, u32[]{:S(2)}) copy-start(s32[32]{0:T(128)} %param.7) | copy-start | bytes 388
  54.2 27.8 %collective-permute-start.2 = (f32[8,2,2,4,3,256]{5,0,4,3,1,2:T(8,128)S(1)}, f32[8,2,2,4,3,256]{5,0,4,3,1,2:T(8,128)S(1)}, u32[]{:S(2)}, u32[]{:S(2)}) collective-permute-start(f32[8,2,2,4,3,256]{5,0,4,3,1,2:T(8,128)S(1)} %get-tuple-element.11), channel_id=1, source_target_pairs={{0,12},{4,8},{8,4},{12,0},{1,13},{5,9},{9,5},{13,1},{2,14},{6,10},... | collective-permute-start | bytes 1179656 | tf_op jit(solution)/shard_map/ppermute | solution.py:41
Sparse Core Ops, SparseCore 0:
  88.1 16.5 reduce-scatter.3
